TPU v7x, 32 devices: a whole 2x2x4 slice. The times are simulated.
32 devices in a mesh: gx: 8 (over z, x), gy: 4 (over y, core).
Axes of the slice: x: 2, y: 2, z: 4, core: 2. Of those that a mesh axis runs over, the one named last changes fastest.
Arguments:
- vectors: float32 [8, 2, 2, 128, 1024], P(None, None, None, 'gx', 'gy'), may hold values from -6 to 6
- bonds: float32 [3, 128, 1024], P(None, 'gx', 'gy'), may hold values from 0.5 to 1.5
- onsite: float32 [2, 128, 1024], P(None, 'gx', 'gy'), may hold values from -1 to 1
Outputs:
- moment_rows: float32 [2, 3, 3, 128], P(None, None, None, 'gx')
- left_last: bfloat16 [8, 2, 2, 128, 1024], P(None, None, None, 'gx', 'gy')
- right_last: bfloat16 [8, 2, 2, 128, 1024], P(None, None, None, 'gx', 'gy')
All inputs are finite; a program needn't handle non-finite values.
Results may differ from a plain program's by a relative error of at most 0.001.
Values sent between devices are 32-bit elements; how exact they have to be, the bound alone decides.
A program may use at most 64 MiB of HBM per device.

v0:
```python
import jax
import jax.numpy as jnp
from jax import lax
from jax.sharding import PartitionSpec as P

VECTORS = 8
MOMENTS = 3


SCALE = 6.0
OFFSETS = (1.0, -0.5, -0.5)
UNITS = (1.0, 1.0, 1.0)


def with_halo(cells, sides, width):
    for axis, dim in sides:
        count = lax.axis_size(axis)
        head = lax.slice_in_dim(cells, 0, width, axis=dim)
        tail = lax.slice_in_dim(cells, cells.shape[dim] - width, cells.shape[dim], axis=dim)
        cells = jnp.concatenate(
            [
                lax.ppermute(tail, axis, [(i, (i + 1) % count) for i in range(count)]),
                cells,
                lax.ppermute(head, axis, [((i + 1) % count, i) for i in range(count)]),
            ],
            axis=dim,
        )
    return cells


def trimmed(array, margin):
    if margin == 0:
        return array
    return array[..., margin:-margin, margin:-margin]


def bond_sums(padded, bond_frame, weights):
    centre = bond_frame[:, 1:-1, 1:-1]
    raised_one = bond_frame[1, 2:, 1:-1]
    raised_two = bond_frame[2, 1:-1, 2:]
    site_a = padded[:, :, 0, 1:-1, 1:-1]
    site_b = padded[:, :, 1, 1:-1, 1:-1]
    into_a = (
        weights[0] * centre[0] * site_b
        + weights[1] * centre[1] * padded[:, :, 1, :-2, 1:-1]
        + weights[2] * centre[2] * padded[:, :, 1, 1:-1, :-2]
    )
    into_b = (
        weights[0] * centre[0] * site_a
        + weights[1] * raised_one * padded[:, :, 0, 2:, 1:-1]
        + weights[2] * raised_two * padded[:, :, 0, 1:-1, 2:]
    )
    return (site_a, site_b, into_a, into_b)


def hamilton(padded, bond_frame, onsite_inner):
    site_a, site_b, into_a, into_b = bond_sums(padded, bond_frame, UNITS)
    return jnp.stack(
        [(onsite_inner[0] * site_a + into_a) / SCALE, (onsite_inner[1] * site_b + into_b) / SCALE],
        axis=2,
    )


def velocity(padded, bond_frame):
    site_a, site_b, sum_a, sum_b = bond_sums(padded, bond_frame, OFFSETS)
    image_a = jnp.stack([sum_a[:, 1], -sum_a[:, 0]], axis=1)
    image_b = jnp.stack([-sum_b[:, 1], sum_b[:, 0]], axis=1)
    return jnp.stack([image_a, image_b], axis=2)


def intersection(left, right):
    real_rows = jnp.sum(left[:, 0] * right[:, 0] + left[:, 1] * right[:, 1], axis=(0, 1, 3))
    imag_rows = jnp.sum(left[:, 0] * right[:, 1] - left[:, 1] * right[:, 0], axis=(0, 1, 3))
    return jnp.stack([real_rows, imag_rows])


def per_device(vectors, bonds, onsite):
    reach = MOMENTS
    stacked_fields = jnp.concatenate([bonds, onsite], axis=0)
    fields = with_halo(stacked_fields, (("gx", 1), ("gy", 2)), reach)
    bond_frame = fields[:3]
    onsite_frame = fields[3:]
    framed = with_halo(vectors, (("gx", 3), ("gy", 4)), reach)

    def apply_hop(field, margin):
        return hamilton(
            field, trimmed(bond_frame, reach - margin), trimmed(onsite_frame, reach - margin + 1)
        )

    def apply_vel(field, margin):
        return velocity(field, trimmed(bond_frame, reach - margin))

    right_chain = [framed]
    for level in range(1, MOMENTS):
        stepped = apply_hop(right_chain[level - 1], reach - level + 1)
        right_chain.append(
            stepped if level == 1 else 2.0 * stepped - trimmed(right_chain[level - 2], 2)
        )
    rights = [
        trimmed(apply_vel(right_chain[level], reach - level), reach - level - 1)
        for level in range(MOMENTS)
    ]
    left_frames = [apply_vel(framed, reach)]
    for level in range(1, MOMENTS):
        stepped = apply_hop(left_frames[level - 1], reach - level)
        left_frames.append(
            stepped if level == 1 else 2.0 * stepped - trimmed(left_frames[level - 2], 2)
        )
    lefts = [trimmed(left_frames[level], reach - 1 - level) for level in range(MOMENTS)]
    divisor = float(VECTORS * vectors.shape[4] * lax.axis_size("gy"))
    partial_block = jnp.stack(
        [
            jnp.stack(
                [intersection(lefts[order], rights[other]) for other in range(MOMENTS)], axis=1
            )
            for order in range(MOMENTS)
        ],
        axis=1,
    )
    moments = lax.psum(partial_block, "gy")
    moments = moments / divisor
    return (moments, lefts[-1].astype(jnp.bfloat16), rights[-1].astype(jnp.bfloat16))


def solution(mesh):
    placed = (P(None, None, None, "gx", "gy"), P(None, "gx", "gy"), P(None, "gx", "gy"))
    return jax.shard_map(
        per_device,
        mesh=mesh,
        in_specs=placed,
        out_specs=(
            P(None, None, None, "gx"),
            P(None, None, None, "gx", "gy"),
            P(None, None, None, "gx", "gy"),
        ),
        check_vma=False,
    )
```

profile of v0, /device:TPU:0, one launch (start us, length us, event | category | flops | bytes accessed | tf_op | source)
XLA Modules:
  0.0 47.4 jit_solution(14140014306718061338)
XLA Ops:
  0.6 0.0 copy-start.1
  0.6 0.0 copy-start.2
  0.7 0.9 %constant_dynamic-update-slice_fusion.1 = f32[5,16,256]{2,1,0:T(8,128)S(1)} fusion(f32[3,16,256]{2,1,0:T(8,128)} %param.4), kind=kLoop, calls=%fused_computation.152 | loop fusion | bytes 98304
  1.5 0.8 %constant_dynamic-update-slice_fusion = f32[5,16,256]{2,1,0:T(8,128)S(1)} fusion(f32[5,16,256]{2,1,0:T(8,128)S(1)} %constant_dynamic-update-slice_fusion.1, f32[2,16,256]{2,1,0:T(8,128)} %param.5), kind=kLoop, calls=%fused_computation.151 | loop fusion | bytes 65536 | tf_op jit(solution)/shard_map/concatenate | solution.py:79
  2.3 3.0 %collective-permute-start = (f32[5,3,256]{2,1,0:T(4,128)S(1)}, f32[5,3,256]{2,1,0:T(4,128)S(1)}, u32[]{:S(2)}, u32[]{:S(2)}) collective-permute-start(f32[5,3,256]{2,1,0:T(4,128)S(1)} %get-tuple-element.103), channel_id=1, source_target_pairs={{0,4},{4,8},{8,12},{12,16},{16,20},{20,24},{24,28},{28,0},{1,5},{5... | collective-permute-start | bytes 46088 | tf_op jit(solution)/shard_map/ppermute | solution.py:22
  5.3 3.1 %collective-permute-start.1 = (f32[5,3,256]{2,1,0:T(4,128)S(1)}, f32[5,3,256]{2,1,0:T(4,128)S(1)}, u32[]{:S(2)}, u32[]{:S(2)}) collective-permute-start(f32[5,3,256]{2,1,0:T(4,128)S(1)} %get-tuple-element.104), channel_id=1, source_target_pairs={{4,0},{8,4},{12,8},{16,12},{20,16},{24,20},{28,24},{0,28},{5,1},{9... | collective-permute-start | bytes 46088 | tf_op jit(solution)/shard_map/ppermute | solution.py:24
  8.4 1.1 %fusion.48 = (f32[8,2,2,3,256]{4,3,2,1,0:T(4,128)S(1)}, f32[8,2,2,3,256]{4,3,2,1,0:T(4,128)S(1)}) fusion(f32[8,2,2,16,256]{4,3,2,1,0:T(8,128)} %param.3), kind=kLoop, calls=%fused_computation.176 | loop fusion | bytes 393216 | tf_op jit(solution)/shard_map/slice | solution.py:18
  9.5 0.1 copy.60
  9.6 0.1 collective-permute-start.4
  9.6 0.1 copy.61
  9.7 4.8 %collective-permute-start.5 = (f32[8,2,2,3,256]{4,0,3,1,2:T(8,128)S(1)}, f32[8,2,2,3,256]{4,0,3,1,2:T(8,128)S(1)}, u32[]{:S(2)}, u32[]{:S(2)}) collective-permute-start(f32[8,2,2,3,256]{4,0,3,1,2:T(8,128)S(1)} %copy.61), channel_id=1, source_target_pairs={{4,0},{8,4},{12,8},{16,12},{20,16},{24,20},{28,24},{0,28},{5,1},{9... | collective-permute-start | bytes 294920 | tf_op jit(solution)/shard_map/ppermute | solution.py:24
  14.4 0.0 copy-done.1
  14.5 0.0 copy-done.2
  14.5 0.0 collective-permute-done
  14.5 0.0 collective-permute-done.1
  14.5 0.1 fusion.52
  14.6 0.0 collective-permute-start.2
  14.6 1.7 %collective-permute-start.3 = (f32[5,22,3]{2,1,0:T(8,128)S(1)}, f32[5,22,3]{2,1,0:T(8,128)S(1)}, u32[]{:S(2)}, u32[]{:S(2)}) collective-permute-start(f32[5,22,3]{2,1,0:T(8,128)S(1)} %get-tuple-element.100), channel_id=1, source_target_pairs={{1,0},{2,1},{3,2},{0,3},{5,4},{6,5},{7,6},{4,7},{9,8},{10,9},{11,1... | collective-permute-start | bytes 3968 | tf_op jit(solution)/shard_map/ppermute | solution.py:24
  16.4 0.0 copy-start
  16.4 1.9 %collective-permute-done.2 = f32[5,22,3]{2,1,0:T(8,128)S(1)} collective-permute-done((f32[5,22,3]{2,1,0:T(8,128)S(1)}, f32[5,22,3]{2,1,0:T(8,128)S(1)}, u32[]{:S(2)}, u32[]{:S(2)}) %collective-permute-start.2) | collective-permute-done | bytes 1352 | tf_op jit(solution)/shard_map/ppermute | solution.py:22
  18.3 0.0 collective-permute-done.3
  18.3 0.2 pad_maximum_fusion.9
  18.5 0.1 broadcast_multiply_fusion.3
  18.6 0.1 broadcast_multiply_fusion.7
  18.7 0.1 slice_bitcast_fusion.6
  18.8 0.1 slice_bitcast_fusion.12
  19.0 0.0 collective-permute-done.4
  19.0 0.0 copy-done
  19.0 0.3 constant_dynamic-update-slice_fusion.3
  19.3 0.0 collective-permute-done.5
  19.3 0.2 fusion.47
  19.5 1.8 %collective-permute-start.6 = (f32[8,2,2,22,3]{4,0,3,1,2:T(8,128)S(1)}, f32[8,2,2,22,3]{4,0,3,1,2:T(8,128)S(1)}, u32[]{:S(2)}, u32[]{:S(2)}) collective-permute-start(f32[8,2,2,22,3]{4,0,3,1,2:T(8,128)S(1)} %get-tuple-element.62), channel_id=1, source_target_pairs={{0,1},{1,2},{2,3},{3,0},{4,5},{5,6},{6,7},{7,4},{8,9},{9,10},{10,1... | collective-permute-start | bytes 25352 | tf_op jit(solution)/shard_map/ppermute | solution.py:22
  21.3 0.0 collective-permute-start.7
  21.4 0.1 broadcast_multiply_fusion.9
  21.4 6.8 %collective-permute-done.6 = f32[8,2,2,22,3]{4,0,3,1,2:T(8,128)S(1)} collective-permute-done((f32[8,2,2,22,3]{4,0,3,1,2:T(8,128)S(1)}, f32[8,2,2,22,3]{4,0,3,1,2:T(8,128)S(1)}, u32[]{:S(2)}, u32[]{:S(2)}) %collective-permute-start.6) | collective-permute-done | bytes 8480 | tf_op jit(solution)/shard_map/ppermute | solution.py:22
  28.3 1.2 %collective-permute-done.7 = f32[8,2,2,22,3]{4,0,3,1,2:T(8,128)S(1)} collective-permute-done((f32[8,2,2,22,3]{4,0,3,1,2:T(8,128)S(1)}, f32[8,2,2,22,3]{4,0,3,1,2:T(8,128)S(1)}, u32[]{:S(2)}, u32[]{:S(2)}) %collective-permute-start.7) | collective-permute-done | bytes 8480 | tf_op jit(solution)/shard_map/ppermute | solution.py:24
  29.4 0.4 pad_maximum_fusion
  29.9 0.7 %fusion.5 = (f32[8,2,20,260]{3,0,2,1:T(8,128)S(1)}, f32[8,2,20,260]{3,0,2,1:T(8,128)S(1)}) fusion(f32[8,2,2,22,262]{4,0,3,1,2:T(8,128)S(1)} %pad_maximum_fusion, f32[20,260]{1,0:T(8,128)S(1)} %get-tuple-element.97, f32[20,260]{1,0:T(8,128)S(1)} %get-tuple-element.94, f32[20,260]{1,0:T(8,128)S(1)} %get-tuple-element.87, f32[20,260]{1,0:T(8,128)S(1)} %get-tuple-element.95, ...), kind=kLoop, calls=%fused_computation.20 | loop fusion | flops 832000 | bytes 2766400 | tf_op jit(solution)/shard_map/add | solution.py:44
  30.6 0.1 slice_negate_fusion
  30.8 0.2 pad_maximum_fusion.8
  31.0 0.7 %add_multiply_fusion.1 = (f32[8,2,1,20,260]{4,0,3,1,2:T(8,128)S(1)}, f32[8,2,1,20,260]{4,0,3,1,2:T(8,128)S(1)}) fusion(f32[8,2,2,22,262]{4,0,3,1,2:T(8,128)S(1)} %pad_maximum_fusion, f32[20,260]{1,0:T(8,128)S(1)} %get-tuple-element.83, f32[20,260]{1,0:T(8,128)S(1)} %get-tuple-element.84, f32[20,260]{1,0:T(8,128)S(1)} %get-tuple-element.87, ...), kind=kLoop, calls=%fused_computation.25 | loop fusion | flops 1331200 | bytes 2808000 | tf_op jit(solution)/shard_map/div | solution.py:59
  31.7 0.5 %bitcast_multiply_fusion.6 = f32[8,2,1,18,258]{4,0,3,2,1:T(8,128)S(1)} fusion(f32[8,2,1,20,260]{4,0,3,1,2:T(8,128)S(1)} %get-tuple-element.47, f32[8,2,1,20,260]{4,0,3,1,2:T(8,128)S(1)} %get-tuple-element.46, f32[18,258]{1,0:T(8,128)S(1)} %get-tuple-element.41, f32[18,258]{1,0:T(8,128)S(1)} %get-tuple-element.90, f32[18,258]{1,0:T(8,128)S(1)} %get-tuple-element.88, ...), kind=kLoop, calls=%fused_computation.40 | loop fusion | flops 594432 | bytes 1560384 | tf_op jit(solution)/shard_map/div | solution.py:59
  32.2 1.0 %fusion.9 = (f32[8,2,1,18,258]{4,0,3,1,2:T(8,128)S(1)}, f32[8,2,1,18,258]{4,0,3,1,2:T(8,128)S(1)}, f32[8,2,1,18,258]{4,0,3,2,1:T(8,128)S(1)}) fusion(f32[8,2,1,20,260]{4,0,3,1,2:T(8,128)S(1)} %maximum_bitcast_fusion, f32[8,2,1,20,260]{4,0,3,1,2:T(8,128)S(1)} %maximum_bitcast_fusion.1, f32[18,258]{1,0:T(8,128)S(1)} %get-tuple-element.41, ...), kind=kLoop, calls=%fused_computation.29 | loop fusion | flops 1783296 | bytes 3993840 | tf_op jit(solution)/shard_map/div | solution.py:59
  33.2 0.3 fusion
  33.5 0.4 fusion.35
  34.1 0.8 %copy.52 = bf16[8,2,2,16,256]{4,3,2,1,0:T(8,128)(2,1)} copy(bf16[8,2,2,16,256]{4,0,3,1,2:T(8,128)(2,1)S(1)} %fusion.1) | data formatting | bytes 524288
  34.9 0.2 pad_maximum_fusion.4
  35.1 0.4 fusion.27
  35.5 0.2 fusion.41
  35.7 0.8 %copy.51 = bf16[8,2,2,16,256]{4,3,2,1,0:T(8,128)(2,1)} copy(bf16[8,2,2,16,256]{4,0,3,1,2:T(8,128)(2,1)S(1)} %get-tuple-element.36) | data formatting | bytes 524288
  36.4 0.6 %fusion.17 = (f32[8,2,18,258]{3,0,2,1:T(8,128)S(1)}, f32[8,2,18,258]{3,0,2,1:T(8,128)S(1)}) fusion(f32[8,2,1,20,260]{4,0,3,1,2:T(8,128)S(1)} %get-tuple-element.46, f32[18,258]{1,0:T(8,128)S(1)} %get-tuple-element.80, f32[18,258]{1,0:T(8,128)S(1)} %get-tuple-element.78, f32[18,258]{1,0:T(8,128)S(1)} %get-tuple-element.93, ...), kind=kLoop, calls=%fused_computation.49 | loop fusion | flops 743040 | bytes 2470608 | tf_op jit(solution)/shard_map/add | solution.py:44
  37.1 0.1 slice_negate_fusion.2
  37.2 0.2 pad_maximum_fusion.5
  37.4 1.1 %add_reduce_fusion.2 = (f32[16]{0:T(128)S(1)}, f32[16]{0:T(128)S(1)}, f32[16]{0:T(128)S(1)}, f32[16]{0:T(128)S(1)}, f32[16]{0:T(128)S(1)}, /*index=5*/f32[16]{0:...) fusion(f32[8,1,2,16,256]{4,0,3,1,2:T(8,128)S(1)} %get-tuple-ele, ...), kind=kLoop, calls=%fused_computation.97 | loop fusion | flops 4259584 | bytes 3146752 | tf_op jit(solution)/shard_map/reduce_sum | solution.py:72
  38.6 0.2 add_reduce_fusion
  39.0 7.8 %psum.7 = f32[2,3,3,16]{3,0,2,1:T(2,128)S(1)} all-reduce(f32[2,3,3,16]{3,0,2,1:T(2,128)S(1)} %pad_maximum_fusion.15), channel_id=1, replica_groups=mesh['gx'=8,'gy'=4] {'gy'}, use_global_device_ids=true, to_apply=%region_18.0 | all-reduce | flops 288 | bytes 2304 | tf_op jit(solution)/shard_map/psum | solution.py:120
  46.8 0.6 %broadcast_multiply_fusion.12 = f32[2,3,3,16]{3,0,2,1:T(2,128)} fusion(f32[2,3,3,16]{3,0,2,1:T(2,128)S(1)} %psum.7), kind=kLoop, calls=%fused_computation.161 | loop fusion | flops 288 | bytes 2304 | tf_op jit(solution)/shard_map/div | solution.py:121
  (30 shorter events, 0.4 us)
Async XLA Ops:
  0.6 13.8 %copy-start.1 = (f32[3,16,256]{2,1,0:T(8,128)S(1)}, f32[3,16,256]{2,1,0:T(8,128)}, u32[]{:S(2)}) copy-start(f32[3,16,256]{2,1,0:T(8,128)} %param.4) | copy-start | bytes 147460
  0.6 13.8 %copy-start.2 = (f32[2,16,256]{2,1,0:T(8,128)S(1)}, f32[2,16,256]{2,1,0:T(8,128)}, u32[]{:S(2)}) copy-start(f32[2,16,256]{2,1,0:T(8,128)} %param.5) | copy-start | bytes 98308
  2.3 12.2 %collective-permute-start = (f32[5,3,256]{2,1,0:T(4,128)S(1)}, f32[5,3,256]{2,1,0:T(4,128)S(1)}, u32[]{:S(2)}, u32[]{:S(2)}) collective-permute-start(f32[5,3,256]{2,1,0:T(4,128)S(1)} %get-tuple-element.103), channel_id=1, source_target_pairs={{0,4},{4,8},{8,12},{12,16},{16,20},{20,24},{24,28},{28,0},{1,5},{5... | collective-permute-start | bytes 46088 | tf_op jit(solution)/shard_map/ppermute | solution.py:22
  5.3 9.2 %collective-permute-start.1 = (f32[5,3,256]{2,1,0:T(4,128)S(1)}, f32[5,3,256]{2,1,0:T(4,128)S(1)}, u32[]{:S(2)}, u32[]{:S(2)}) collective-permute-start(f32[5,3,256]{2,1,0:T(4,128)S(1)} %get-tuple-element.104), channel_id=1, source_target_pairs={{4,0},{8,4},{12,8},{16,12},{20,16},{24,20},{28,24},{0,28},{5,1},{9... | collective-permute-start | bytes 46088 | tf_op jit(solution)/shard_map/ppermute | solution.py:24
  9.6 9.4 %collective-permute-start.4 = (f32[8,2,2,3,256]{4,0,3,1,2:T(8,128)S(1)}, f32[8,2,2,3,256]{4,0,3,1,2:T(8,128)S(1)}, u32[]{:S(2)}, u32[]{:S(2)}) collective-permute-start(f32[8,2,2,3,256]{4,0,3,1,2:T(8,128)S(1)} %copy.60), channel_id=1, source_target_pairs={{0,4},{4,8},{8,12},{12,16},{16,20},{20,24},{24,28},{28,0},{1,5},{5... | collective-permute-start | bytes 294920 | tf_op jit(solution)/shard_map/ppermute | solution.py:22
  9.7 9.6 %collective-permute-start.5 = (f32[8,2,2,3,256]{4,0,3,1,2:T(8,128)S(1)}, f32[8,2,2,3,256]{4,0,3,1,2:T(8,128)S(1)}, u32[]{:S(2)}, u32[]{:S(2)}) collective-permute-start(f32[8,2,2,3,256]{4,0,3,1,2:T(8,128)S(1)} %copy.61), channel_id=1, source_target_pairs={{4,0},{8,4},{12,8},{16,12},{20,16},{24,20},{28,24},{0,28},{5,1},{9... | collective-permute-start | bytes 294920 | tf_op jit(solution)/shard_map/ppermute | solution.py:24
  14.6 3.7 %collective-permute-start.2 = (f32[5,22,3]{2,1,0:T(8,128)S(1)}, f32[5,22,3]{2,1,0:T(8,128)S(1)}, u32[]{:S(2)}, u32[]{:S(2)}) collective-permute-start(f32[5,22,3]{2,1,0:T(8,128)S(1)} %get-tuple-element.99), channel_id=1, source_target_pairs={{0,1},{1,2},{2,3},{3,0},{4,5},{5,6},{6,7},{7,4},{8,9},{9,10},{10,1... | collective-permute-start | bytes 3968 | tf_op jit(solution)/shard_map/ppermute | solution.py:22
  14.6 3.6 %collective-permute-start.3 = (f32[5,22,3]{2,1,0:T(8,128)S(1)}, f32[5,22,3]{2,1,0:T(8,128)S(1)}, u32[]{:S(2)}, u32[]{:S(2)}) collective-permute-start(f32[5,22,3]{2,1,0:T(8,128)S(1)} %get-tuple-element.100), channel_id=1, source_target_pairs={{1,0},{2,1},{3,2},{0,3},{5,4},{6,5},{7,6},{4,7},{9,8},{10,9},{11,1... | collective-permute-start | bytes 3968 | tf_op jit(solution)/shard_map/ppermute | solution.py:24
  16.4 2.6 %copy-start = (f32[8,2,2,16,256]{4,3,2,1,0:T(8,128)S(1)}, f32[8,2,2,16,256]{4,3,2,1,0:T(8,128)}, u32[]{:S(2)}) copy-start(f32[8,2,2,16,256]{4,3,2,1,0:T(8,128)} %param.3) | copy-start | bytes 1572868
  19.5 8.8 %collective-permute-start.6 = (f32[8,2,2,22,3]{4,0,3,1,2:T(8,128)S(1)}, f32[8,2,2,22,3]{4,0,3,1,2:T(8,128)S(1)}, u32[]{:S(2)}, u32[]{:S(2)}) collective-permute-start(f32[8,2,2,22,3]{4,0,3,1,2:T(8,128)S(1)} %get-tuple-element.62), channel_id=1, source_target_pairs={{0,1},{1,2},{2,3},{3,0},{4,5},{5,6},{6,7},{7,4},{8,9},{9,10},{10,1... | collective-permute-start | bytes 25352 | tf_op jit(solution)/shard_map/ppermute | solution.py:22
  21.3 8.1 %collective-permute-start.7 = (f32[8,2,2,22,3]{4,0,3,1,2:T(8,128)S(1)}, f32[8,2,2,22,3]{4,0,3,1,2:T(8,128)S(1)}, u32[]{:S(2)}, u32[]{:S(2)}) collective-permute-start(f32[8,2,2,22,3]{4,0,3,1,2:T(8,128)S(1)} %get-tuple-element.63), channel_id=1, source_target_pairs={{1,0},{2,1},{3,2},{0,3},{5,4},{6,5},{7,6},{4,7},{9,8},{10,9},{11,1... | collective-permute-start | bytes 25352 | tf_op jit(solution)/shard_map/ppermute | solution.py:24
where the time goes:
time: 47.7 us; the launch traced here: 47.4 us
  starting transfers between devices  14.6 us (31%)
  waiting for transfers between devices  9.9 us (21%)
  other arithmetic  8.93 us (19%)
  blocking collectives  7.8 us (16%)
  local copies, waits for them, and re-layouts  5.19 us (11%)
  between operations  1.05 us (2%)
    ppermute x4, starting transfers between devices, with_halo(): lax.ppermute(head, axis, [((i + 1) % count, i) for i in range(count)])  9.64 us
    ppermute x4, waiting for transfers between devices, with_halo(): lax.ppermute(tail, axis, [(i, (i + 1) % count) for i in range(count)])  8.72 us
    psum x1, blocking collectives, per_device(): moments = lax.psum(partial_block, 'gy')  7.8 us
    ppermute x4, starting transfers between devices, with_halo(): lax.ppermute(tail, axis, [(i, (i + 1) % count) for i in range(count)])  4.92 us
    unnamed x13, local copies, waits for them, and re-layouts  2.83 us
    div x3, other arithmetic, hamilton(): (onsite_inner[1] * site_b + into_b) / SCALE  2.26 us
    add x3, other arithmetic, bond_sums(): weights[0] * centre[0] * site_b  1.76 us
    reduce_sum x2, other arithmetic, intersection(): jnp.sum(left[:, 0] * right[:, 0] + left[:, 1] * right[:, 1], axis=(0, 1, 3))  1.36 us
  transfers between devices with their start and end apart: 8, of which 3 were waited for; matrix products, arithmetic and copies ran while one was open for 5% of the time, Pallas kernels for 0%

commit v1 on v0

v1 whole, which is shorter than its diff:
```python
import functools
import jax
import jax.numpy as jnp
from jax import lax
from jax.experimental import pallas as pl
from jax.experimental.pallas import tpu as pltpu
from jax.sharding import PartitionSpec as P

MOMENTS = 3
SCALE = 6.0
EDGE = 2
GROUP = 4
HALF = 64
LANES = 128
MESH = pl.DeviceIdType.MESH


def bond_terms(a, b, fields, left, right, up, down):
    b0, b1, b2, b1d, b2r = fields
    return b0 * b, b1 * up(b) + b2 * left(b), b0 * a, b1d * down(a) + b2r * right(a)


def kernel(
    gxn, gyn, vec, bonds, onsite, out_mom, out_left, out_right,
    x, f, fd, c_own, c_left, c_right, halo_f, halo_x, keep, acc, part_mom, lbuf, rbuf,
    load_sem, send_sem, recv_sem, msend_sem, mrecv_sem, out_sem,
):
    vectors, _, _, rows, cols = vec.shape
    tall = x.shape[3]
    tiles = cols // LANES
    last = rows - EDGE
    gx = lax.axis_index("gx")
    gy = lax.axis_index("gy")

    def peer(dx, dy):
        return (lax.rem(gx + dx + gxn, gxn), lax.rem(gy + dy + gyn, gyn))

    barrier = pltpu.get_barrier_semaphore()
    near = [(dx % gxn, dy % gyn) for dx in (-1, 0, 1) for dy in (-1, 0, 1)]
    near += [(0, dy) for dy in range(gyn)]
    near = sorted(set(near) - {(0, 0)})
    for dx, dy in near:
        pl.semaphore_signal(barrier, inc=1, device_id=peer(dx, dy), device_id_type=MESH)

    loads = [
        pltpu.make_async_copy(vec, x.at[:, :, :, 0:rows, :], load_sem.at[0]),
        pltpu.make_async_copy(bonds, f.at[0:3, 0:rows, :], load_sem.at[1]),
        pltpu.make_async_copy(onsite, f.at[3:5, 0:rows, :], load_sem.at[2]),
    ]
    for copy in loads:
        copy.start()
    pl.semaphore_wait(barrier, len(near))

    sends = []

    def send(src, dst, dx, dy):
        n = len(sends)
        copy = pltpu.make_async_remote_copy(
            src_ref=src, dst_ref=dst, send_sem=send_sem.at[n], recv_sem=recv_sem.at[n],
            device_id=peer(dx, dy), device_id_type=MESH,
        )
        copy.start()
        sends.append(copy)

    below = slice(rows, rows + EDGE)
    send(vec.at[:, :, 0, 0:2, :], x.at[:, :, 0, rows : rows + 2, :], -1, 0)
    send(vec.at[:, :, 1, rows - 2 : rows, :], x.at[:, :, 1, tall - 2 : tall, :], 1, 0)
    send(vec.at[:, :, 1, 0:1, :], x.at[:, :, 1, rows : rows + 1, :], -1, 0)
    send(vec.at[:, :, 0, rows - 1 : rows, :], x.at[:, :, 0, tall - 1 : tall, :], 1, 0)
    send(bonds.at[:, 0:2, :], f.at[0:3, rows : rows + 2, :], -1, 0)
    send(bonds.at[:, rows - 2 : rows, :], f.at[0:3, tall - 2 : tall, :], 1, 0)
    send(onsite.at[:, 0:2, :], f.at[3:5, rows : rows + 2, :], -1, 0)
    send(onsite.at[:, rows - 2 : rows, :], f.at[3:5, tall - 2 : tall, :], 1, 0)

    for copy in loads:
        copy.wait()

    lane = lax.broadcasted_iota(jnp.int32, (rows, LANES), 1)
    spot = lax.rem(lane, HALF)

    def packed(items):
        total = jnp.zeros((rows, LANES), jnp.float32)
        for k, (first, final) in enumerate(items):
            both = jnp.where(lane < HALF, first, final)
            moved = pltpu.roll(both, GROUP * k + EDGE, 1)
            total = jnp.where(spot // GROUP == k, moved, total) if k else moved
        total = jnp.where(lane < HALF, total, pltpu.roll(total, HALF, 1))
        return total

    def edges(ref, *index):
        return ref[(*index, slice(0, rows), slice(0, LANES))], ref[
            (*index, slice(0, rows), slice(cols - LANES, cols))
        ]

    for sub in range(2):
        c_own[sub, 0:rows] = packed(
            [edges(x, v, p, sub) for v in range(vectors) for p in range(2)]
        )
    c_own[2, 0:rows] = packed([edges(f, k) for k in range(5)])

    core = slice(0, rows)
    send(c_own.at[:, core, :], c_right.at[:, core, :], 0, -1)
    send(c_own.at[:, core, :], c_left.at[:, core, :], 0, 1)
    top, bottom = c_own.at[:, 0:EDGE, :], c_own.at[:, last:rows, :]
    past, ahead = slice(rows, rows + EDGE), slice(tall - EDGE, tall)
    send(top, c_own.at[:, past, :], -1, 0)
    send(top, c_right.at[:, past, :], -1, -1)
    send(top, c_left.at[:, past, :], -1, 1)
    send(bottom, c_own.at[:, ahead, :], 1, 0)
    send(bottom, c_right.at[:, ahead, :], 1, -1)
    send(bottom, c_left.at[:, ahead, :], 1, 1)

    acc[...] = jnp.zeros_like(acc)
    for copy in sends:
        copy.wait_recv()

    tlane = lax.broadcasted_iota(jnp.int32, (tall, LANES), 1)
    tspot = lax.rem(tlane, GROUP)
    from_left = (tlane < HALF) & (tspot < EDGE)
    from_right = (tlane >= HALF) & (tspot >= EDGE)

    def joined(k):
        return jnp.where(
            from_left, c_left[k], jnp.where(from_right, c_right[k], c_own[k])
        )

    def up(t):
        return pltpu.roll(t, 1, 0)

    def down(t):
        return pltpu.roll(t, t.shape[0] - 1, 0)

    field_tile = joined(2)
    tgroup = lax.rem(tlane, HALF)
    for k in range(5):
        t = pltpu.roll(field_tile, LANES - GROUP * k, 1) if k else field_tile
        t = jnp.where(tgroup < GROUP, t, 0.0)
        step = GROUP
        while step < HALF:
            t = t + pltpu.roll(t, step, 1)
            step *= 2
        halo_f[k] = t
    halo_f[5] = down(halo_f[1])
    halo_f[6] = pltpu.roll(halo_f[2], LANES - 1, 1)

    lane_last = tlane == LANES - 1
    lane_first = tlane == 0

    def tile(t):
        return slice(t * LANES, (t + 1) * LANES)

    for t in range(tiles):
        fd[0, :, tile(t)] = down(f[1, :, tile(t)])
    after = pltpu.roll(halo_f[2], LANES - 1 - (HALF + EDGE), 1)
    for t in reversed(range(tiles)):
        turned = pltpu.roll(f[2, :, tile(t)], LANES - 1, 1)
        fd[1, :, tile(t)] = jnp.where(lane_last, after, turned)
        after = turned

    sixth = 1.0 / SCALE

    def h_fields(width=tall):
        return tuple(halo_f[k] for k in (0, 1, 2, 5, 6))

    h_on = (halo_f[3], halo_f[4])

    def h_terms(a, b):
        return bond_terms(
            a, b, h_fields(), lambda t: pltpu.roll(t, 1, 1),
            lambda t: pltpu.roll(t, LANES - 1, 1), up, down,
        )

    def energy(a, b, terms, on, factor):
        a0, a12, b0, b12 = terms
        return (on[0] * a + (a0 + a12)) * factor, (on[1] * b + (b0 + b12)) * factor

    def speed(terms):
        a0, a12, b0, b12 = terms
        return a0 - 0.5 * a12, 0.5 * b12 - b0

    q0 = (joined(0), joined(1))
    t0 = h_terms(*q0)
    q1 = energy(*q0, t0, h_on, sixth)
    m0 = speed(t0)
    h1 = energy(*q1, h_terms(*q1), h_on, 2.0 * sixth)
    q2 = (h1[0] - q0[0], h1[1] - q0[1])
    m1 = energy(*m0, h_terms(*m0), h_on, sixth)
    for k, pair in enumerate((q0, q1, q2, m0, m1)):
        halo_x[k, 0], halo_x[k, 1] = pair

    short = slice(0, rows)

    def one_vector(v, carry):
        for part in range(2):
            turn_b = lax.rem(2 * LANES - (GROUP * (2 * v + part) + 1), LANES)
            turn_a = lax.rem(3 * LANES - 1 - (HALF + GROUP * (2 * v + part) + EDGE), LANES)

            def terms(pair, k, cut):
                a, b = pair
                rim_b = pltpu.roll(halo_x[k, 1], turn_b, 1)
                rim_a = pltpu.roll(halo_x[k, 0], turn_a, 1)
                keep_rows = (lambda t: t[0:rows]) if cut else (lambda t: t)
                first, final = keep_rows(lane_first), keep_rows(lane_last)
                size = short if cut else slice(0, tall)
                b_turn = [pltpu.roll(keep_rows(t), 1, 1) for t in b]
                a_turn = [pltpu.roll(keep_rows(t), LANES - 1, 1) for t in a]
                found = []
                for t in range(tiles):
                    prev = keep_rows(rim_b) if t == 0 else b_turn[t - 1]
                    nxt = keep_rows(rim_a) if t == tiles - 1 else a_turn[t + 1]
                    left = jnp.where(first, prev, b_turn[t])
                    right = jnp.where(final, nxt, a_turn[t])
                    a0 = f[0, size, tile(t)] * keep_rows(b[t])
                    a12 = f[1, size, tile(t)] * keep_rows(up(b[t])) + f[2, size, tile(t)] * left
                    b0 = f[0, size, tile(t)] * keep_rows(a[t])
                    b12 = fd[0, size, tile(t)] * keep_rows(down(a[t])) + fd[1, size, tile(t)] * right
                    found.append((a0, a12, b0, b12))
                return found

            def stepped(pair, found, factor, cut, minus=None):
                a_new, b_new = [], []
                size = short if cut else slice(0, tall)
                for t in range(tiles):
                    on = (f[3, size, tile(t)], f[4, size, tile(t)])
                    a, b = energy(pair[0][t][size], pair[1][t][size], found[t], on, factor)
                    if minus is not None:
                        a, b = a - minus[0][t][size], b - minus[1][t][size]
                    a_new.append(a)
                    b_new.append(b)
                return a_new, b_new

            def moved(found):
                both = [speed(item) for item in found]
                return [item[0] for item in both], [item[1] for item in both]

            def store(slot, pair):
                for sub in range(2):
                    for t in range(tiles):
                        keep[slot, part, sub, :, tile(t)] = pair[sub][t][0:rows]

            q0 = tuple([x[v, part, sub, :, tile(t)] for t in range(tiles)] for sub in range(2))
            t0 = terms(q0, 0, False)
            m0 = moved(t0)
            store(0, m0)
            q1 = stepped(q0, t0, sixth, False)
            t1 = terms(q1, 1, False)
            store(3, moved(t1))
            q2 = stepped(q1, t1, 2.0 * sixth, False, q0)
            n2 = moved(terms(q2, 2, True))
            store(4, n2)
            m1 = stepped(m0, terms(m0, 3, False), sixth, False)
            store(1, m1)
            m2 = stepped(m1, terms(m1, 4, True), 2.0 * sixth, True, m0)
            store(2, m2)
            for sub in range(2):
                for t in range(tiles):
                    for buf, pair in ((lbuf, m2), (rbuf, n2)):
                        value = pair[sub][t]
                        value = -value if part == 0 else value
                        buf[v, 1 - part, sub, :, tile(t)] = value.astype(jnp.bfloat16)

        for r in range(0, rows, 8):
            band = slice(r, r + 8)
            sums = [[[acc[p, n, m, band, :] for m in range(MOMENTS)] for n in range(MOMENTS)] for p in range(2)]
            for sub in range(2):
                for t in range(tiles):
                    at = [[keep[s, p, sub, band, tile(t)] for p in range(2)] for s in range(5)]
                    for n in range(MOMENTS):
                        for m in range(MOMENTS):
                            left = at[n]
                            right = at[0] if m == 0 else at[2 + m]
                            sums[0][n][m] = sums[0][n][m] + (left[0] * right[0] + left[1] * right[1])
                            sums[1][n][m] = sums[1][n][m] + (left[0] * right[1] - left[1] * right[0])
            for p in range(2):
                for n in range(MOMENTS):
                    for m in range(MOMENTS):
                        acc[p, n, m, band, :] = sums[p][n][m]
        return carry

    lax.fori_loop(0, vectors, one_vector, 0)

    outs = [
        pltpu.make_async_copy(lbuf, out_left, out_sem.at[0]),
        pltpu.make_async_copy(rbuf, out_right, out_sem.at[1]),
    ]
    for copy in outs:
        copy.start()

    count = 2 * MOMENTS * MOMENTS * rows
    part_mom[0] = lax.dot_general(
        jnp.ones((8, LANES), jnp.float32), acc[...].reshape(count, LANES),
        (((1,), (1,)), ((), ())), precision=lax.Precision.HIGHEST,
        preferred_element_type=jnp.float32,
    )
    swaps = []
    for d in range(1, gyn):
        copy = pltpu.make_async_remote_copy(
            src_ref=part_mom.at[0], dst_ref=part_mom.at[d],
            send_sem=msend_sem.at[d - 1], recv_sem=mrecv_sem.at[d - 1],
            device_id=peer(0, d), device_id_type=MESH,
        )
        copy.start()
        swaps.append(copy)
    for copy in swaps:
        copy.wait_recv()
    total = part_mom[0]
    for d in range(1, gyn):
        total = total + part_mom[d]
    total = total / float(vectors * cols * gyn)
    for p in range(2):
        for n in range(MOMENTS):
            for m in range(MOMENTS):
                k = (p * MOMENTS + n) * MOMENTS + m
                out_mom[p, n, m : m + 1, :] = total[0:1, k * rows : (k + 1) * rows]
    for copy in sends + swaps:
        copy.wait_send()
    for copy in outs:
        copy.wait()


def solution(mesh):
    gxn, gyn = mesh.shape["gx"], mesh.shape["gy"]

    def per_device(vectors, bonds, onsite):
        count, _, _, rows, cols = vectors.shape
        tall = rows + 8
        f32 = jnp.float32
        any_space = pl.BlockSpec(memory_space=pl.ANY)
        last = jax.ShapeDtypeStruct(vectors.shape, jnp.bfloat16)
        sends = 16
        return pl.pallas_call(
            functools.partial(kernel, gxn, gyn),
            out_shape=(
                jax.ShapeDtypeStruct((2, MOMENTS, MOMENTS, rows), f32), last, last,
            ),
            in_specs=[any_space] * 3,
            out_specs=(pl.BlockSpec(memory_space=pltpu.VMEM), any_space, any_space),
            scratch_shapes=[
                pltpu.VMEM((count, 2, 2, tall, cols), f32),
                pltpu.VMEM((5, tall, cols), f32),
                pltpu.VMEM((2, tall, cols), f32),
                pltpu.VMEM((3, tall, LANES), f32),
                pltpu.VMEM((3, tall, LANES), f32),
                pltpu.VMEM((3, tall, LANES), f32),
                pltpu.VMEM((7, tall, LANES), f32),
                pltpu.VMEM((5, 2, tall, LANES), f32),
                pltpu.VMEM((5, 2, 2, rows, cols), f32),
                pltpu.VMEM((2, MOMENTS, MOMENTS, rows, LANES), f32),
                pltpu.VMEM((gyn, 8, 2 * MOMENTS * MOMENTS * rows), f32),
                pltpu.VMEM(vectors.shape, jnp.bfloat16),
                pltpu.VMEM(vectors.shape, jnp.bfloat16),
                pltpu.SemaphoreType.DMA((3,)),
                pltpu.SemaphoreType.DMA((sends,)),
                pltpu.SemaphoreType.DMA((sends,)),
                pltpu.SemaphoreType.DMA((gyn - 1,)),
                pltpu.SemaphoreType.DMA((gyn - 1,)),
                pltpu.SemaphoreType.DMA((2,)),
            ],
            compiler_params=pltpu.CompilerParams(collective_id=0, has_side_effects=True),
        )(vectors, bonds, onsite)

    return jax.shard_map(
        per_device,
        mesh=mesh,
        in_specs=(P(None, None, None, "gx", "gy"), P(None, "gx", "gy"), P(None, "gx", "gy")),
        out_specs=(
            P(None, None, None, "gx"),
            P(None, None, None, "gx", "gy"),
            P(None, None, None, "gx", "gy"),
        ),
        check_vma=False,
    )
```

time: 47.7 us -> 22.6 us (0.47)
  Pallas kernels: 0 us -> 17.9 us
  starting transfers between devices: 14.6 us -> 0 us
  waiting for transfers between devices: 9.9 us -> 0 us
  other arithmetic: 8.93 us -> 0 us
  blocking collectives: 7.8 us -> 0 us
  local copies, waits for them, and re-layouts: 5.19 us -> 3.73 us
    pallas_call x0 -> x1, Pallas kernels: none -> 17.9 us  [per_device(): pl.pallas_call(functools.partial(kernel, gxn, gyn), out_shape=(jax.ShapeD...]
    ppermute x8 -> x0, starting transfers between devices: 14.6 us -> none  [the longest x4 9.64 us: with_halo(): lax.ppermute(head, axis, [((i + 1) % count, i) for i in range(count)])]
    ppermute x8 -> x0, waiting for transfers between devices: 9.9 us -> none  [the longest x4 8.72 us: with_halo(): lax.ppermute(tail, axis, [(i, (i + 1) % count) for i in range(count)])]
    psum x1 -> x0, blocking collectives: 7.8 us -> none  [per_device(): moments = lax.psum(partial_block, 'gy')]
    div x5 -> x0, other arithmetic: 3.28 us -> none  [the longest x3 2.26 us: hamilton(): (onsite_inner[1] * site_b + into_b) / SCALE]
    add x3 -> x0, other arithmetic: 1.76 us -> none  [bond_sums(): weights[0] * centre[0] * site_b]
    reduce_sum x2 -> x0, other arithmetic: 1.36 us -> none  [intersection(): jnp.sum(left[:, 0] * right[:, 0] + left[:, 1] * right[:, 1], axis=(0, 1, 3))]
    slice x4 -> x0, local copies, waits for them, and re-layouts: 1.33 us -> none  [the longest x1 1.08 us: with_halo(): head = lax.slice_in_dim(cells, 0, width, axis=dim)]
  transfers between devices with their start and end apart: 8 -> 0, of which waited for: 3 -> 0; matrix products, arithmetic and copies ran while one was open for 5% -> 0% of each run, Pallas kernels for 0% -> 0%
where the time goes in v1:
time: 22.6 us; the launch traced here: 22.3 us
  Pallas kernels  17.9 us (79%)
  local copies, waits for them, and re-layouts  3.73 us (17%)
  between operations  0.64 us (3%)
    pallas_call x1, Pallas kernels, per_device(): pl.pallas_call(functools.partial(kernel, gxn, gyn), out_shape=(jax.ShapeD...  17.9 us
    unnamed x4, local copies, waits for them, and re-layouts  2.42 us
    pallas_call x1, local copies, waits for them, and re-layouts, per_device(): pl.pallas_call(functools.partial(kernel, gxn, gyn), out_shape=(jax.ShapeD...  1.31 us

profile of v1, /device:TPU:0, one launch (start us, length us, event | category | flops | bytes accessed | tf_op | source)
XLA Modules:
  0.0 22.3 jit_solution(10197645596393215014)
XLA Ops:
  0.6 17.9 %shard_map.58 = (f32[2,3,3,16]{3,2,1,0:T(4,128)}, bf16[8,2,2,16,256]{4,3,2,1,0:T(8,128)(2,1)}, bf16[8,2,2,16,256]{4,3,2,1,0:T(8,128)(2,1)}) custom-call(f32[8,2,2,16,256]{4,3,2,1,0:T(8,128)} %vec.1, f32[3,16,256]{2,1,0:T(8,128)} %bonds.1, f32[2,16,256]{2,1,0:T(8,128)} %onsite.1), custom_call_target="tpu_custom_call" | custom-call | tf_op jit(solution)/shard_map/pallas_call | solution.py:331
  18.6 1.3 %copy.6 = f32[2,3,3,16]{3,0,2,1:T(2,128)} copy(f32[2,3,3,16]{3,2,1,0:T(4,128)} %get-tuple-element.3) | data formatting | bytes 2304 | tf_op jit(solution)/shard_map/pallas_call | solution.py:331
  19.9 0.0 copy-start
  19.9 1.7 %copy.9 = bf16[8,2,2,16,256]{4,3,2,1,0:T(8,128)(2,1)} copy(bf16[8,2,2,16,256]{4,3,2,1,0:T(8,128)(2,1)} %get-tuple-element.10) | data formatting | bytes 524288
  21.6 0.0 copy-done
  21.6 0.7 %copy.10 = bf16[8,2,2,16,256]{4,3,2,1,0:T(8,128)(2,1)} copy(bf16[8,2,2,16,256]{4,3,2,1,0:T(8,128)(2,1)S(1)} %copy-done) | data formatting | bytes 524288
Async XLA Ops:
  19.9 1.7 %copy-start = (bf16[8,2,2,16,256]{4,3,2,1,0:T(8,128)(2,1)S(1)}, bf16[8,2,2,16,256]{4,3,2,1,0:T(8,128)(2,1)}, u32[]{:S(2)}) copy-start(bf16[8,2,2,16,256]{4,3,2,1,0:T(8,128)(2,1)} %get-tuple-element.11) | copy-start | bytes 786436

commit v2 on v1

--- a/solution.py
+++ b/solution.py
@@ -12,6 +12,7 @@
 GROUP = 4
 HALF = 64
 LANES = 128
+GRANT = 16 * 1024 * 1024
 MESH = pl.DeviceIdType.MESH
 
 
@@ -21,9 +22,9 @@
 
 
 def kernel(
-    gxn, gyn, vec, bonds, onsite, out_mom, out_left, out_right,
-    x, f, fd, c_own, c_left, c_right, halo_f, halo_x, keep, acc, part_mom, lbuf, rbuf,
-    load_sem, send_sem, recv_sem, msend_sem, mrecv_sem, out_sem,
+    gxn, gyn, vec, bonds, onsite, out_mom, lbuf, rbuf,
+    x, f, fd, c_own, c_left, c_right, halo_f, halo_x, keep, acc, part_mom,
+    load_sem, send_sem, recv_sem, msend_sem, mrecv_sem,
 ):
     vectors, _, _, rows, cols = vec.shape
     tall = x.shape[3]
@@ -49,8 +50,6 @@
     ]
     for copy in loads:
         copy.start()
-    pl.semaphore_wait(barrier, len(near))
-
     sends = []
 
     def send(src, dst, dx, dy):
@@ -62,18 +61,19 @@
         copy.start()
         sends.append(copy)
 
-    below = slice(rows, rows + EDGE)
-    send(vec.at[:, :, 0, 0:2, :], x.at[:, :, 0, rows : rows + 2, :], -1, 0)
-    send(vec.at[:, :, 1, rows - 2 : rows, :], x.at[:, :, 1, tall - 2 : tall, :], 1, 0)
-    send(vec.at[:, :, 1, 0:1, :], x.at[:, :, 1, rows : rows + 1, :], -1, 0)
-    send(vec.at[:, :, 0, rows - 1 : rows, :], x.at[:, :, 0, tall - 1 : tall, :], 1, 0)
-    send(bonds.at[:, 0:2, :], f.at[0:3, rows : rows + 2, :], -1, 0)
-    send(bonds.at[:, rows - 2 : rows, :], f.at[0:3, tall - 2 : tall, :], 1, 0)
-    send(onsite.at[:, 0:2, :], f.at[3:5, rows : rows + 2, :], -1, 0)
-    send(onsite.at[:, rows - 2 : rows, :], f.at[3:5, tall - 2 : tall, :], 1, 0)
-
     for copy in loads:
         copy.wait()
+
+    acc[...] = jnp.zeros_like(acc)
+    pl.semaphore_wait(barrier, len(near))
+
+    core = slice(0, rows)
+    send(x.at[:, :, 0, 0:2, :], x.at[:, :, 0, rows : rows + 2, :], -1, 0)
+    send(x.at[:, :, 1, rows - 2 : rows, :], x.at[:, :, 1, tall - 2 : tall, :], 1, 0)
+    send(x.at[:, :, 1, 0:1, :], x.at[:, :, 1, rows : rows + 1, :], -1, 0)
+    send(x.at[:, :, 0, rows - 1 : rows, :], x.at[:, :, 0, tall - 1 : tall, :], 1, 0)
+    send(f.at[:, 0:2, :], f.at[:, rows : rows + 2, :], -1, 0)
+    send(f.at[:, rows - 2 : rows, :], f.at[:, tall - 2 : tall, :], 1, 0)
 
     lane = lax.broadcasted_iota(jnp.int32, (rows, LANES), 1)
     spot = lax.rem(lane, HALF)
@@ -98,7 +98,6 @@
         )
     c_own[2, 0:rows] = packed([edges(f, k) for k in range(5)])
 
-    core = slice(0, rows)
     send(c_own.at[:, core, :], c_right.at[:, core, :], 0, -1)
     send(c_own.at[:, core, :], c_left.at[:, core, :], 0, 1)
     top, bottom = c_own.at[:, 0:EDGE, :], c_own.at[:, last:rows, :]
@@ -110,7 +109,6 @@
     send(bottom, c_right.at[:, ahead, :], 1, -1)
     send(bottom, c_left.at[:, ahead, :], 1, 1)
 
-    acc[...] = jnp.zeros_like(acc)
     for copy in sends:
         copy.wait_recv()
 
@@ -279,13 +277,6 @@
 
     lax.fori_loop(0, vectors, one_vector, 0)
 
-    outs = [
-        pltpu.make_async_copy(lbuf, out_left, out_sem.at[0]),
-        pltpu.make_async_copy(rbuf, out_right, out_sem.at[1]),
-    ]
-    for copy in outs:
-        copy.start()
-
     count = 2 * MOMENTS * MOMENTS * rows
     part_mom[0] = lax.dot_general(
         jnp.ones((8, LANES), jnp.float32), acc[...].reshape(count, LANES),
@@ -295,7 +286,7 @@
     swaps = []
     for d in range(1, gyn):
         copy = pltpu.make_async_remote_copy(
-            src_ref=part_mom.at[0], dst_ref=part_mom.at[d],
+            src_ref=part_mom.at[0, 0:1], dst_ref=part_mom.at[d, 0:1],
             send_sem=msend_sem.at[d - 1], recv_sem=mrecv_sem.at[d - 1],
             device_id=peer(0, d), device_id_type=MESH,
         )
@@ -306,14 +297,24 @@
     total = part_mom[0]
     for d in range(1, gyn):
         total = total + part_mom[d]
-    total = total / float(vectors * cols * gyn)
+    out_mom[...] = total / float(vectors * cols * gyn)
+    for copy in sends + swaps:
+        copy.wait_send()
+
+
+def writer(total, lbuf, rbuf, out_mom, out_left, out_right, out_sem):
+    outs = [
+        pltpu.make_async_copy(lbuf, out_left, out_sem.at[0]),
+        pltpu.make_async_copy(rbuf, out_right, out_sem.at[1]),
+    ]
+    for copy in outs:
+        copy.start()
+    rows = out_mom.shape[3]
     for p in range(2):
         for n in range(MOMENTS):
             for m in range(MOMENTS):
                 k = (p * MOMENTS + n) * MOMENTS + m
-                out_mom[p, n, m : m + 1, :] = total[0:1, k * rows : (k + 1) * rows]
-    for copy in sends + swaps:
-        copy.wait_send()
+                out_mom[n, m, p : p + 1, :] = total[0:1, k * rows : (k + 1) * rows]
     for copy in outs:
         copy.wait()
 
@@ -325,16 +326,20 @@
         count, _, _, rows, cols = vectors.shape
         tall = rows + 8
         f32 = jnp.float32
-        any_space = pl.BlockSpec(memory_space=pl.ANY)
+        in_hbm = pl.BlockSpec(memory_space=pltpu.HBM)
         last = jax.ShapeDtypeStruct(vectors.shape, jnp.bfloat16)
         sends = 16
-        return pl.pallas_call(
+        in_vmem = pl.BlockSpec(memory_space=pltpu.VMEM)
+        sums = (8, 2 * MOMENTS * MOMENTS * rows)
+        made = pl.pallas_call(
             functools.partial(kernel, gxn, gyn),
             out_shape=(
-                jax.ShapeDtypeStruct((2, MOMENTS, MOMENTS, rows), f32), last, last,
+                pltpu.VMEM(sums, f32),
+                pltpu.VMEM(vectors.shape, jnp.bfloat16),
+                pltpu.VMEM(vectors.shape, jnp.bfloat16),
             ),
-            in_specs=[any_space] * 3,
-            out_specs=(pl.BlockSpec(memory_space=pltpu.VMEM), any_space, any_space),
+            in_specs=[in_hbm] * 3,
+            out_specs=(in_vmem,) * 3,
             scratch_shapes=[
                 pltpu.VMEM((count, 2, 2, tall, cols), f32),
                 pltpu.VMEM((5, tall, cols), f32),
@@ -346,18 +351,29 @@
                 pltpu.VMEM((5, 2, tall, LANES), f32),
                 pltpu.VMEM((5, 2, 2, rows, cols), f32),
                 pltpu.VMEM((2, MOMENTS, MOMENTS, rows, LANES), f32),
-                pltpu.VMEM((gyn, 8, 2 * MOMENTS * MOMENTS * rows), f32),
-                pltpu.VMEM(vectors.shape, jnp.bfloat16),
-                pltpu.VMEM(vectors.shape, jnp.bfloat16),
+                pltpu.VMEM((gyn, *sums), f32),
                 pltpu.SemaphoreType.DMA((3,)),
                 pltpu.SemaphoreType.DMA((sends,)),
                 pltpu.SemaphoreType.DMA((sends,)),
                 pltpu.SemaphoreType.DMA((gyn - 1,)),
                 pltpu.SemaphoreType.DMA((gyn - 1,)),
-                pltpu.SemaphoreType.DMA((2,)),
             ],
-            compiler_params=pltpu.CompilerParams(collective_id=0, has_side_effects=True),
-        )(vectors, bonds, onsite)
+            compiler_params=pltpu.CompilerParams(
+                collective_id=0, has_side_effects=True, vmem_limit_bytes=GRANT
+            ),
+        )(*(pltpu.with_memory_space_constraint(array, pltpu.HBM) for array in (vectors, bonds, onsite)))
+        made = [pltpu.with_memory_space_constraint(array, pltpu.VMEM) for array in made]
+        moments, left, right = pl.pallas_call(
+            writer,
+            out_shape=(
+                jax.ShapeDtypeStruct((MOMENTS, MOMENTS, 2, rows), f32), last, last,
+            ),
+            in_specs=[in_vmem] * 3,
+            out_specs=(in_vmem, in_hbm, in_hbm),
+            scratch_shapes=[pltpu.SemaphoreType.DMA((2,))],
+            compiler_params=pltpu.CompilerParams(vmem_limit_bytes=GRANT),
+        )(*made)
+        return jnp.transpose(moments, (2, 0, 1, 3)), left, right
 
     return jax.shard_map(
         per_device,

time: 22.6 us -> 19.1 us (0.85)
  local copies, waits for them, and re-layouts: 3.73 us -> 0 us
  Pallas kernels: 17.9 us -> 18.3 us
    unnamed x4 -> x0, local copies, waits for them, and re-layouts: 2.42 us -> none
    pallas_call x1 -> x0, local copies, waits for them, and re-layouts: 1.31 us -> none  [per_device(): pl.pallas_call(functools.partial(kernel, gxn, gyn), out_shape=(jax.ShapeD...]
    pallas_call x1 -> x2, Pallas kernels: 17.9 us -> 18.3 us  [the longest x1 16.9 us: per_device(): pl.pallas_call(functools.partial(kernel, gxn, gyn), out_shape=(pltpu.VMEM...]
where the time goes in v2:
time: 19.1 us; the launch traced here: 19 us
  Pallas kernels  18.3 us (96%)
  between operations  0.64 us (3%)
    pallas_call x1, Pallas kernels, per_device(): pl.pallas_call(functools.partial(kernel, gxn, gyn), out_shape=(pltpu.VMEM...  16.9 us
    pallas_call x1, Pallas kernels, per_device(): pl.pallas_call(writer, out_shape=(jax.ShapeDtypeStruct((MOMENTS, MOMENTS,...  1.41 us

profile of v2, /device:TPU:0, one launch (start us, length us, event | category | flops | bytes accessed | tf_op | source)
XLA Modules:
  0.0 19.0 jit_solution(5710641165112129449)
XLA Ops:
  0.6 16.9 %shard_map.58 = (f32[8,288]{1,0:T(8,128)S(1)}, bf16[8,2,2,16,256]{4,3,2,1,0:T(8,128)(2,1)S(1)}, bf16[8,2,2,16,256]{4,3,2,1,0:T(8,128)(2,1)S(1)}) custom-call(f32[8,2,2,16,256]{4,3,2,1,0:T(8,128)} %vec.1, f32[3,16,256]{2,1,0:T(8,128)} %bonds.1, f32[2,16,256]{2,1,0:T(8,128)} %onsite.1), custom_call_target="tpu_custom_call" | custom-call | tf_op jit(solution)/shard_map/pallas_call | solution.py:334
  17.5 1.4 %shard_map.59 = (f32[3,3,2,16]{3,2,1,0:T(2,128)}, bf16[8,2,2,16,256]{4,3,2,1,0:T(8,128)(2,1)}, bf16[8,2,2,16,256]{4,3,2,1,0:T(8,128)(2,1)}) custom-call(f32[8,288]{1,0:T(8,128)S(1)} %get-tuple-element.9.total, bf16[8,2,2,16,256]{4,3,2,1,0:T(8,128)(2,1)S(1)} %get-tuple-element.10.lbuf, bf16[8,2,2,16,256]{4,3,2,1,0:T(8,128)(2,1)S(1)} %get-tuple-element.11.rbuf), custom_call_target="tpu_custom_call" | custom-call | tf_op jit(solution)/shard_map/pallas_call | solution.py:366

commit v3 on v2

--- a/solution.py
+++ b/solution.py
@@ -23,7 +23,7 @@
 
 def kernel(
     gxn, gyn, vec, bonds, onsite, out_mom, lbuf, rbuf,
-    x, f, fd, c_own, c_left, c_right, halo_f, halo_x, keep, acc, part_mom,
+    x, f, fd, g, c_own, c_left, c_right, halo_f, halo_x, keep, acc, part_mom,
     load_sem, send_sem, recv_sem, msend_sem, mrecv_sem,
 ):
     vectors, _, _, rows, cols = vec.shape
@@ -156,6 +156,15 @@
         after = turned
 
     sixth = 1.0 / SCALE
+    half_square = 0.5 * SCALE * SCALE
+    for t in range(tiles):
+        raw = [f[i, :, tile(t)] for i in range(3)] + [fd[i, :, tile(t)] for i in range(2)]
+        raw += [f[i, :, tile(t)] for i in (3, 4)]
+        for i, item in enumerate(raw):
+            g[0, i, :, tile(t)] = item * sixth
+            g[1, i, :, tile(t)] = item * (2.0 * sixth)
+            if i < 5:
+                g[2, i, :, tile(t)] = item * ((-0.5 if i in (1, 2, 3, 4) else 1.0) / half_square)
 
     def h_fields(width=tall):
         return tuple(halo_f[k] for k in (0, 1, 2, 5, 6))
@@ -178,10 +187,10 @@
 
     q0 = (joined(0), joined(1))
     t0 = h_terms(*q0)
-    q1 = energy(*q0, t0, h_on, sixth)
+    q1 = energy(*q0, t0, h_on, 1.0)
     m0 = speed(t0)
-    h1 = energy(*q1, h_terms(*q1), h_on, 2.0 * sixth)
-    q2 = (h1[0] - q0[0], h1[1] - q0[1])
+    h1 = energy(*q1, h_terms(*q1), h_on, 1.0)
+    q2 = (h1[0] - half_square * q0[0], h1[1] - half_square * q0[1])
     m1 = energy(*m0, h_terms(*m0), h_on, sixth)
     for k, pair in enumerate((q0, q1, q2, m0, m1)):
         halo_x[k, 0], halo_x[k, 1] = pair
@@ -193,7 +202,7 @@
             turn_b = lax.rem(2 * LANES - (GROUP * (2 * v + part) + 1), LANES)
             turn_a = lax.rem(3 * LANES - 1 - (HALF + GROUP * (2 * v + part) + EDGE), LANES)
 
-            def terms(pair, k, cut):
+            def terms(pair, k, cut, w=None):
                 a, b = pair
                 rim_b = pltpu.roll(halo_x[k, 1], turn_b, 1)
                 rim_a = pltpu.roll(halo_x[k, 0], turn_a, 1)
@@ -208,21 +217,34 @@
                     nxt = keep_rows(rim_a) if t == tiles - 1 else a_turn[t + 1]
                     left = jnp.where(first, prev, b_turn[t])
                     right = jnp.where(final, nxt, a_turn[t])
-                    a0 = f[0, size, tile(t)] * keep_rows(b[t])
-                    a12 = f[1, size, tile(t)] * keep_rows(up(b[t])) + f[2, size, tile(t)] * left
-                    b0 = f[0, size, tile(t)] * keep_rows(a[t])
-                    b12 = fd[0, size, tile(t)] * keep_rows(down(a[t])) + fd[1, size, tile(t)] * right
+                    if w is None:
+                        f0, f1, f2 = (f[i, size, tile(t)] for i in range(3))
+                        d1, d2 = fd[0, size, tile(t)], fd[1, size, tile(t)]
+                    else:
+                        f0, f1, f2, d1, d2 = (g[w, i, size, tile(t)] for i in range(5))
+                    a0 = f0 * keep_rows(b[t])
+                    a12 = f1 * keep_rows(up(b[t])) + f2 * left
+                    b0 = f0 * keep_rows(a[t])
+                    b12 = d1 * keep_rows(down(a[t])) + d2 * right
                     found.append((a0, a12, b0, b12))
                 return found
 
-            def stepped(pair, found, factor, cut, minus=None):
+            def stepped(pair, found, cut, w=None, minus=None, times=None):
                 a_new, b_new = [], []
                 size = short if cut else slice(0, tall)
                 for t in range(tiles):
-                    on = (f[3, size, tile(t)], f[4, size, tile(t)])
-                    a, b = energy(pair[0][t][size], pair[1][t][size], found[t], on, factor)
+                    if w is None:
+                        on = (f[3, size, tile(t)], f[4, size, tile(t)])
+                    else:
+                        on = (g[w, 5, size, tile(t)], g[w, 6, size, tile(t)])
+                    a0, a12, b0, b12 = found[t]
+                    a = on[0] * pair[0][t][size] + (a0 + a12)
+                    b = on[1] * pair[1][t][size] + (b0 + b12)
                     if minus is not None:
-                        a, b = a - minus[0][t][size], b - minus[1][t][size]
+                        less = [minus[i][t][size] for i in range(2)]
+                        if times is not None:
+                            less = [item * times for item in less]
+                        a, b = a - less[0], b - less[1]
                     a_new.append(a)
                     b_new.append(b)
                 return a_new, b_new
@@ -240,15 +262,18 @@
             t0 = terms(q0, 0, False)
             m0 = moved(t0)
             store(0, m0)
-            q1 = stepped(q0, t0, sixth, False)
+            q1 = stepped(q0, t0, False)
             t1 = terms(q1, 1, False)
             store(3, moved(t1))
-            q2 = stepped(q1, t1, 2.0 * sixth, False, q0)
-            n2 = moved(terms(q2, 2, True))
+            q2 = stepped(q1, t1, False, None, q0, half_square)
+            n2 = [[], []]
+            for a0, a12, b0, b12 in terms(q2, 2, True, 2):
+                n2[0].append(a0 + a12)
+                n2[1].append(-(b0 + b12))
             store(4, n2)
-            m1 = stepped(m0, terms(m0, 3, False), sixth, False)
+            m1 = stepped(m0, terms(m0, 3, False, 0), False, 0)
             store(1, m1)
-            m2 = stepped(m1, terms(m1, 4, True), 2.0 * sixth, True, m0)
+            m2 = stepped(m1, terms(m1, 4, True, 1), True, 1, m0)
             store(2, m2)
             for sub in range(2):
                 for t in range(tiles):
@@ -277,6 +302,9 @@
 
     lax.fori_loop(0, vectors, one_vector, 0)
 
+    for p in range(2):
+        for n in range(MOMENTS):
+            acc[p, n, 1] = acc[p, n, 1] * sixth
     count = 2 * MOMENTS * MOMENTS * rows
     part_mom[0] = lax.dot_general(
         jnp.ones((8, LANES), jnp.float32), acc[...].reshape(count, LANES),
@@ -344,6 +372,7 @@
                 pltpu.VMEM((count, 2, 2, tall, cols), f32),
                 pltpu.VMEM((5, tall, cols), f32),
                 pltpu.VMEM((2, tall, cols), f32),
+                pltpu.VMEM((3, 7, tall, cols), f32),
                 pltpu.VMEM((3, tall, LANES), f32),
                 pltpu.VMEM((3, tall, LANES), f32),
                 pltpu.VMEM((3, tall, LANES), f32),

time: 19.1 us -> 19 us (level)
  no operation moved by 1% of the time
where the time goes in v3:
time: 19 us; the launch traced here: 18.8 us
  Pallas kernels  18.2 us (96%)
  between operations  0.64 us (3%)
    pallas_call x1, Pallas kernels, per_device(): pl.pallas_call(functools.partial(kernel, gxn, gyn), out_shape=(pltpu.VMEM...  16.8 us
    pallas_call x1, Pallas kernels, per_device(): pl.pallas_call(writer, out_shape=(jax.ShapeDtypeStruct((MOMENTS, MOMENTS,...  1.41 us

profile of v3, /device:TPU:0, one launch (start us, length us, event | category | flops | bytes accessed | tf_op | source)
XLA Modules:
  0.0 18.8 jit_solution(17368620299874176892)
XLA Ops:
  0.6 16.8 %shard_map.58 = (f32[8,288]{1,0:T(8,128)S(1)}, bf16[8,2,2,16,256]{4,3,2,1,0:T(8,128)(2,1)S(1)}, bf16[8,2,2,16,256]{4,3,2,1,0:T(8,128)(2,1)S(1)}) custom-call(f32[8,2,2,16,256]{4,3,2,1,0:T(8,128)} %vec.1, f32[3,16,256]{2,1,0:T(8,128)} %bonds.1, f32[2,16,256]{2,1,0:T(8,128)} %onsite.1), custom_call_target="tpu_custom_call" | custom-call | tf_op jit(solution)/shard_map/pallas_call | solution.py:362
  17.4 1.4 %shard_map.59 = (f32[3,3,2,16]{3,2,1,0:T(2,128)}, bf16[8,2,2,16,256]{4,3,2,1,0:T(8,128)(2,1)}, bf16[8,2,2,16,256]{4,3,2,1,0:T(8,128)(2,1)}) custom-call(f32[8,288]{1,0:T(8,128)S(1)} %get-tuple-element.9.total, bf16[8,2,2,16,256]{4,3,2,1,0:T(8,128)(2,1)S(1)} %get-tuple-element.10.lbuf, bf16[8,2,2,16,256]{4,3,2,1,0:T(8,128)(2,1)S(1)} %get-tuple-element.11.rbuf), custom_call_target="tpu_custom_call" | custom-call | tf_op jit(solution)/shard_map/pallas_call | solution.py:395

commit v4 on v3

--- a/solution.py
+++ b/solution.py
@@ -109,7 +109,23 @@
     send(bottom, c_right.at[:, ahead, :], 1, -1)
     send(bottom, c_left.at[:, ahead, :], 1, 1)
 
-    for copy in sends:
+    def scaled(i, t, item):
+        g[0, i, :, tile(t)] = item * (1.0 / SCALE)
+        g[1, i, :, tile(t)] = item * (2.0 / SCALE)
+        if i < 5:
+            g[2, i, :, tile(t)] = item * ((-1.0 if i else 2.0) / (SCALE * SCALE))
+
+    def tile(t):
+        return slice(t * LANES, (t + 1) * LANES)
+
+    for copy in sends[4:6]:
+        copy.wait_recv()
+    for t in range(tiles):
+        fd[0, :, tile(t)] = pltpu.roll(f[1, :, tile(t)], tall - 1, 0)
+        for i, item in ((0, f[0, :, tile(t)]), (1, f[1, :, tile(t)]), (2, f[2, :, tile(t)]),
+                        (3, fd[0, :, tile(t)]), (5, f[3, :, tile(t)]), (6, f[4, :, tile(t)])):
+            scaled(i, t, item)
+    for copy in sends[:4] + sends[6:]:
         copy.wait_recv()
 
     tlane = lax.broadcasted_iota(jnp.int32, (tall, LANES), 1)
@@ -147,8 +163,6 @@
     def tile(t):
         return slice(t * LANES, (t + 1) * LANES)
 
-    for t in range(tiles):
-        fd[0, :, tile(t)] = down(f[1, :, tile(t)])
     after = pltpu.roll(halo_f[2], LANES - 1 - (HALF + EDGE), 1)
     for t in reversed(range(tiles)):
         turned = pltpu.roll(f[2, :, tile(t)], LANES - 1, 1)
@@ -158,13 +172,7 @@
     sixth = 1.0 / SCALE
     half_square = 0.5 * SCALE * SCALE
     for t in range(tiles):
-        raw = [f[i, :, tile(t)] for i in range(3)] + [fd[i, :, tile(t)] for i in range(2)]
-        raw += [f[i, :, tile(t)] for i in (3, 4)]
-        for i, item in enumerate(raw):
-            g[0, i, :, tile(t)] = item * sixth
-            g[1, i, :, tile(t)] = item * (2.0 * sixth)
-            if i < 5:
-                g[2, i, :, tile(t)] = item * ((-0.5 if i in (1, 2, 3, 4) else 1.0) / half_square)
+        scaled(4, t, fd[1, :, tile(t)])
 
     def h_fields(width=tall):
         return tuple(halo_f[k] for k in (0, 1, 2, 5, 6))

time: 19 us -> 19 us (level)
  no operation moved by 1% of the time
where the time goes in v4:
time: 19 us; the launch traced here: 18.8 us
  Pallas kernels  18.2 us (96%)
  between operations  0.64 us (3%)
    pallas_call x1, Pallas kernels, per_device(): pl.pallas_call(functools.partial(kernel, gxn, gyn), out_shape=(pltpu.VMEM...  16.8 us
    pallas_call x1, Pallas kernels, per_device(): pl.pallas_call(writer, out_shape=(jax.ShapeDtypeStruct((MOMENTS, MOMENTS,...  1.41 us

profile of v4, /device:TPU:0, one launch (start us, length us, event | category | flops | bytes accessed | tf_op | source)
XLA Modules:
  0.0 18.8 jit_solution(15524659747923477126)
XLA Ops:
  0.6 16.8 %shard_map.58 = (f32[8,288]{1,0:T(8,128)S(1)}, bf16[8,2,2,16,256]{4,3,2,1,0:T(8,128)(2,1)S(1)}, bf16[8,2,2,16,256]{4,3,2,1,0:T(8,128)(2,1)S(1)}) custom-call(f32[8,2,2,16,256]{4,3,2,1,0:T(8,128)} %vec.1, f32[3,16,256]{2,1,0:T(8,128)} %bonds.1, f32[2,16,256]{2,1,0:T(8,128)} %onsite.1), custom_call_target="tpu_custom_call" | custom-call | tf_op jit(solution)/shard_map/pallas_call | solution.py:370
  17.4 1.4 %shard_map.59 = (f32[3,3,2,16]{3,2,1,0:T(2,128)}, bf16[8,2,2,16,256]{4,3,2,1,0:T(8,128)(2,1)}, bf16[8,2,2,16,256]{4,3,2,1,0:T(8,128)(2,1)}) custom-call(f32[8,288]{1,0:T(8,128)S(1)} %get-tuple-element.9.total, bf16[8,2,2,16,256]{4,3,2,1,0:T(8,128)(2,1)S(1)} %get-tuple-element.10.lbuf, bf16[8,2,2,16,256]{4,3,2,1,0:T(8,128)(2,1)S(1)} %get-tuple-element.11.rbuf), custom_call_target="tpu_custom_call" | custom-call | tf_op jit(solution)/shard_map/pallas_call | solution.py:403
